TPU v7x, 256 devices: a whole 4x4x8 slice. The times are simulated.
256 devices in a mesh: expert: 32 (over z_hi, y, core), dp: 8 (over z_lo, x).
Axes of the slice: x: 4, y: 4, z: 8 (z_hi: 4, z_lo: 2; z = z_hi * 2 + z_lo), core: 2. Of those that a mesh axis runs over, the one named last changes fastest.
Arguments:
- tokens: bfloat16 [32768, 4096], P(('expert', 'dp')), may hold values from -6 to 6
- route: int32 [32768, 2], P(('expert', 'dp')), may hold values from 0 to 63, all different within a row; in each aligned block of 128 rows (0 to 127, 128 to 255, ...) at most 12 rows name the same one
- gate_output_gradient: bfloat16 [32768, 2, 1536], P(('expert', 'dp')), may hold values from -0.4375 to 0.4375
- frozen_gate_weight: bfloat16 [64, 4096, 1536], P('expert', 'dp'), may hold values from -0.09375 to 0.09375
- adapter_first: bfloat16 [64, 4096, 16], P('expert'), may hold values from -0.09375 to 0.09375
- adapter_second: bfloat16 [64, 16, 1536], P('expert'), may hold values from -0.15625 to 0.15625
Outputs:
- grad_a: float32 [64, 4096, 16], P('expert')
- grad_b: float32 [64, 16, 1536], P('expert')
Inputs may be any that keep to these rules, and one draw needn't show every extreme that they name: `route`: each row names 2 different experts. Within each device's aligned block of 128 rows no expert is named more than 12 times.
All inputs are finite; a program needn't handle non-finite values.
Results may differ from a plain program's by a relative error of at most 0.0043.
Values may be sent and summed in bfloat16 or wider, within the bound.
No kernel may reach another device: no remote copies, remote signals or barrier semaphores. Data moves between devices by JAX's collectives and lax.ppermute only.
A program may use at most 128 MiB of HBM per device.

v0:
```python
import jax
import jax.numpy as jnp
from jax import lax
from jax.experimental import pallas as pl
from jax.experimental.pallas import tpu as pltpu
from jax.sharding import Mesh, PartitionSpec as P


ADAPTER_SCALE = 2.0
EXPERT_AXES = ("zh", "y", "c")
DP_AXES = ("zl", "x")


def dot(a, b, dims=((1,), (0,))):
    return lax.dot_general(a, b, (dims, ((), ())), preferred_element_type=jnp.float32)


def silu_slope(gate_preactivation):
    squash = jax.nn.sigmoid(gate_preactivation)
    return squash * (1.0 + gate_preactivation * (1.0 - squash))


def slot_targets(route, cap):
    rows, top = route.shape
    flat = route.T.reshape(rows * top)
    before = jnp.arange(rows * top)[:, None] > jnp.arange(rows * top)[None, :]
    same = flat[:, None] == flat[None, :]
    ranks = jnp.sum((same & before).astype(jnp.int32), axis=1)
    return (flat * cap + ranks).reshape(top, rows)


RIGHT = [(i, (i + 1) % 4) for i in range(4)]
LEFT = [(i, (i - 1) % 4) for i in range(4)]


def first_hop(shard):
    return lax.ppermute(shard, "x", RIGHT), lax.ppermute(shard, "x", LEFT)


def second_hop(before, after):
    half = before.shape[0] // 2
    return lax.ppermute(before[:half], "x", RIGHT), lax.ppermute(after[half:], "x", LEFT)


def join_weights(where_ref, pieces, weight):
    x, zl = where_ref[0], where_ref[1]
    rows = weight.shape[0] // 8

    @pl.when(pl.program_id(0) == 0)
    def _():
        for n, piece in enumerate(pieces):
            line = zl if n < 4 else 1 - zl
            at = pl.multiple_of((line * 4 + (x + (0, 3, 1, 2)[n % 4]) % 4) * rows, rows)
            weight[pl.ds(at, rows), :] = piece[...]


def half_kernel(where_ref, x_ref, first_ref, *refs):
    frozen_ref, low_ref, weight = refs[8:]
    join_weights(where_ref, refs[:8], weight)
    frozen_ref[...] = dot(x_ref[...], weight[...])
    low_ref[...] = dot(x_ref[...], first_ref[...], ((1,), (1,)))


def final_kernel(where_ref, xa_ref, xb_ref, g_ref, frozen_ref, lowa_ref, first_ref, second_ref, *refs):
    out_ref, frozen_acc, slope_acc, sums, weight = refs[8:]
    join_weights(where_ref, refs[:8], weight)
    step = pl.program_id(0)
    low = (lowa_ref[...] + dot(xb_ref[...], first_ref[...], ((1,), (1,)))).astype(jnp.bfloat16)
    frozen_acc[...] = frozen_ref[...] + dot(xb_ref[...], weight[...])
    half = g_ref.shape[1] // 2
    for h in range(2):
        cols = slice(h * half, (h + 1) * half)
        preact = frozen_acc[:, cols] + ADAPTER_SCALE * dot(low, second_ref[:, cols])
        slope = g_ref[:, cols].astype(jnp.float32) * silu_slope(preact)
        slope_acc[:, cols] = slope.astype(jnp.bfloat16)
    back = dot(slope_acc[...], second_ref[...], ((1,), (1,))).astype(jnp.bfloat16)

    @pl.when(step == 0)
    def _():
        sums[...] = jnp.zeros_like(sums)

    width = xa_ref.shape[1] // 8
    for h, x_ref in enumerate((xa_ref, xb_ref)):
        part = dot(back, x_ref[...], ((0,), (0,)))
        for n in range(8):
            at = (2 * n + h) * width
            sums[:, at : at + width] += part[:, n * width : (n + 1) * width]
    sums[:, 16 * width :] += dot(low, slope_acc[...], ((0,), (0,)))

    @pl.when(step == pl.num_programs(0) - 1)
    def _():
        chunk = out_ref.shape[2]
        for n in range(4):
            out_ref[n] = ADAPTER_SCALE * sums[:, n * chunk : (n + 1) * chunk]


ROW_BLOCK = 256


def row_spec(array):
    return pl.BlockSpec((ROW_BLOCK, array.shape[1]), lambda i, w: (i, 0))


def whole_spec(array):
    return pl.BlockSpec(array.shape, lambda i, w: (0, 0))


def piece_specs(pieces, h):
    specs = []
    for piece in pieces:
        at = h if piece.shape[0] == 512 else 0
        specs.append(pl.BlockSpec((256, piece.shape[1]), lambda i, w, at=at: (at, 0)))
    return specs


def half_products(where, x, first, pieces, h):
    rows, hidden, rank = x.shape[0], pieces[0].shape[1], first.shape[0]
    return pl.pallas_call(
        half_kernel,
        grid_spec=pltpu.PrefetchScalarGridSpec(
            num_scalar_prefetch=1,
            grid=(rows // ROW_BLOCK,),
            in_specs=[row_spec(x), whole_spec(first)] + piece_specs(pieces, h),
            out_specs=[
                pl.BlockSpec((ROW_BLOCK, hidden), lambda i, w: (i, 0)),
                pl.BlockSpec((ROW_BLOCK, rank), lambda i, w: (i, 0)),
            ],
            scratch_shapes=[pltpu.VMEM((x.shape[1], hidden), jnp.bfloat16)],
        ),
        cost_estimate=pl.CostEstimate(
            flops=2 * rows * x.shape[1] * hidden, bytes_accessed=14 * 2**20, transcendentals=0
        ),
        out_shape=[
            jax.ShapeDtypeStruct((rows, hidden), jnp.float32),
            jax.ShapeDtypeStruct((rows, rank), jnp.float32),
        ],
        name="half_products",
    )(where, x, first, *pieces)


def gradients(where, xa, xb, g, frozen, low, first, second, pieces, h):
    rows, hidden, rank = xa.shape[0], pieces[0].shape[1], first.shape[0]
    total = 2 * xa.shape[1] + hidden
    by_row = [row_spec(v) for v in (xa, xb, g, frozen, low)]
    return pl.pallas_call(
        final_kernel,
        grid_spec=pltpu.PrefetchScalarGridSpec(
            num_scalar_prefetch=1,
            grid=(rows // ROW_BLOCK,),
            in_specs=by_row + [whole_spec(first), whole_spec(second)] + piece_specs(pieces, h),
            out_specs=pl.BlockSpec((4, rank, total // 4), lambda i, w: (0, 0, 0)),
            scratch_shapes=[
                pltpu.VMEM((ROW_BLOCK, hidden), jnp.float32),
                pltpu.VMEM((ROW_BLOCK, hidden), jnp.bfloat16),
                pltpu.VMEM((rank, total), jnp.float32),
                pltpu.VMEM((xa.shape[1], hidden), jnp.bfloat16),
            ],
        ),
        out_shape=jax.ShapeDtypeStruct((4, rank, total // 4), jnp.float32),
        name="gradients",
    )(where, xa, xb, g, frozen, low, first, second, *pieces)


def split_kernel(tokens_ref, *out_refs):
    for h, out_ref in enumerate(out_refs):
        for n in range(out_ref.shape[1] // 256):
            at = (2 * n + h) * 256
            out_ref[:, n * 256 : (n + 1) * 256] = tokens_ref[:, at : at + 256]


def split_columns(tokens):
    shape = jax.ShapeDtypeStruct((tokens.shape[0], tokens.shape[1] // 2), tokens.dtype)
    return pl.pallas_call(split_kernel, out_shape=[shape, shape], name="split_columns")(tokens)


def local(tokens, route, gate_output_gradient, frozen_gate_weight, adapter_first, adapter_second):
    tok_rows, width = tokens.shape
    hidden = gate_output_gradient.shape[2]
    cap = 12
    depth = 8
    zh, zl, x = lax.axis_index("zh"), lax.axis_index("zl"), lax.axis_index("x")
    half_width = width // 2

    lines = [
        lax.all_gather(part, ("zh", "zl"), axis=0, tiled=True) for part in split_columns(tokens)
    ]

    target = slot_targets(route, cap)
    line_target = jnp.broadcast_to(target[None], (depth, 2, tok_rows))
    line_target = lax.all_to_all(line_target, ("zh", "zl"), split_axis=0, concat_axis=0, tiled=True)

    mine = lax.dynamic_index_in_dim(frozen_gate_weight, zl, 0, keepdims=False)
    other = lax.dynamic_index_in_dim(frozen_gate_weight, 1 - zl, 0, keepdims=False)
    near = first_hop(mine)
    other, line_target = lax.optimization_barrier((other, line_target))
    got = lax.ppermute(other, "zl", [(0, 1), (1, 0)])

    row = jnp.arange(depth * depth * cap, dtype=jnp.int32)
    outer, inner, rank = row // (depth * cap), row // cap % depth, row % cap
    zi = zh * 2 + zl
    ahead = (zi + inner) % depth
    key = ((ahead // 2 * depth + outer) * 2 + ahead % 2) * cap + rank
    pick_g = key[:, None] == target.reshape(1, 2 * tok_rows)
    slots = jnp.concatenate([gate_output_gradient[:, k] for k in range(2)], axis=0)
    send_g = dot(pick_g.astype(jnp.bfloat16), slots).astype(jnp.bfloat16)
    send_g = send_g.reshape(depth, depth * cap, hidden)
    send_g, line_target = lax.optimization_barrier((send_g, line_target))
    column_g = lax.all_to_all(send_g, ("y", "c"), split_axis=0, concat_axis=0, tiled=True)
    swapped = (inner * depth + outer) * cap + rank
    swap = (swapped[:, None] == row[None, :]).astype(jnp.bfloat16)
    column_g = dot(swap, column_g.reshape(-1, hidden)).astype(jnp.bfloat16)

    line_target = line_target.transpose(1, 0, 2).reshape(2, depth * tok_rows)
    served = (zh * depth + outer) * 2 + zl
    key = (served * cap + row % cap)[:, None]
    col = jnp.arange(depth * tok_rows, dtype=jnp.int32)
    same_block = (row // cap % depth)[:, None] == (col // tok_rows)[None, :]
    pick = same_block & ((line_target[0][None] == key) | (line_target[1][None] == key))
    pick = pick.astype(jnp.bfloat16)

    def packed(line):
        return dot(pick, line).astype(jnp.bfloat16).reshape(depth, depth * cap, half_width)

    def spread(rows):
        rows = lax.all_to_all(rows, ("y", "c"), split_axis=0, concat_axis=0, tiled=True)
        return rows.reshape(depth * depth * cap, half_width)

    near_opposite = second_hop(*near)
    got, near_opposite, column_g = lax.optimization_barrier((got, near_opposite, column_g))
    far = first_hop(got)
    line0, near_opposite = lax.optimization_barrier((lines[0], near_opposite))
    xa = spread(packed(line0))
    far_opposite = second_hop(*far)
    blocks_g = [column_g[n * depth * cap : (n + 1) * depth * cap] for n in range(depth)]
    line1, far_opposite, blocks_g = lax.optimization_barrier((lines[1], far_opposite, blocks_g))
    for n in (4, 5, 3, 6, 2, 7, 1):
        moves = [(i, (i + n) % depth) for i in range(depth)]
        blocks_g[n] = lax.ppermute(blocks_g[n], ("zh", "zl"), moves)
    xb = spread(packed(line1))

    behind = (zi - inner) % depth
    order = (behind * depth + outer) * cap + rank
    order = (order[:, None] == row[None, :]).astype(jnp.bfloat16)
    rows_g = dot(order, jnp.concatenate(blocks_g, axis=0)).astype(jnp.bfloat16)

    first = lax.dynamic_index_in_dim(adapter_first, zl, 0, keepdims=False)
    second = lax.dynamic_index_in_dim(adapter_second, zl, 0, keepdims=False)
    first = first.T
    first_a, first_b = (
        jnp.concatenate([first[:, at : at + 256] for at in range(256 * h, width, 512)], axis=1)
        for h in range(2)
    )
    where = jnp.stack([x, zl]).astype(jnp.int32)
    pieces = [
        [mine, *near, near_opposite[h], got, *far, far_opposite[h]]
        for h in range(2)
    ]
    frozen, low = half_products(where, xa, first_a, pieces[0], 0)
    parts = gradients(where, xa, xb, rows_g, frozen, low, first_b, second, pieces[1], 1)

    rank, chunk = parts.shape[1:]
    parts = lax.all_to_all(parts, "x", split_axis=0, concat_axis=0, tiled=True)
    total = jnp.sum(parts, axis=0).astype(jnp.bfloat16)
    total = jnp.broadcast_to(total[None], (8, rank, chunk))
    total = lax.all_to_all(total, DP_AXES, split_axis=0, concat_axis=0, tiled=True)
    total = total.reshape(2, 4, rank, chunk).transpose(0, 2, 1, 3).reshape(2, rank, 4 * chunk)
    grad_a = total[:, :, :width].transpose(0, 2, 1).astype(jnp.float32)
    return grad_a, total[:, :, width:].astype(jnp.float32)


def solution(mesh):
    fine = Mesh(mesh.devices.reshape(4, 4, 2, 2, 4), EXPERT_AXES + DP_AXES)
    everyone = EXPERT_AXES + DP_AXES

    def step(*args):
        return local(*args)

    step = jax.shard_map(
        step,
        mesh=fine,
        in_specs=(
            P(everyone, None),
            P(everyone, None),
            P(everyone, None, None),
            P(EXPERT_AXES, DP_AXES, None),
            P(EXPERT_AXES, None, None),
            P(EXPERT_AXES, None, None),
        ),
        out_specs=(P(EXPERT_AXES, None, None), P(EXPERT_AXES, None, None)),
        check_vma=False,
    )
    return step
```

profile of v0, /device:TPU:8, one launch (start us, length us, event | category | flops | bytes accessed | tf_op | source)
XLA Modules:
  0.0 301.2 jit_solution(5961381637269277564)
XLA Ops:
  7.2 2.3 split_columns.1
  11.8 8.5 %all-to-all-start = ((s32[8,2,128]{2,1,0:T(2,128)}), s32[8,2,128]{2,1,0:T(2,128)S(1)}, u32[]{:S(2)}, u32[]{:S(2)}) async-start(s32[8,2,128]{2,1,0:T(2,128)} %broadcast_in_dim.4), calls=%async_computation | async-start | bytes 16384 | tf_op jit(solution)/shard_map/all_to_all | solution.py:190
  21.7 3.3 %dynamic-slice_bitcast_fusion = (bf16[512,1536]{1,0:T(8,128)(2,1)S(1)}, bf16[512,1536]{1,0:T(8,128)(2,1)}) fusion(bf16[2,512,1536]{2,1,0:T(8,128)(2,1)} %param.9, s32[]{:T(128)S(6)} %select_n.160, s32[]{:T(128)S(6)} %select_n.159), kind=kLoop, calls=%fused_computation.8 | loop fusion | bytes 6291464 | tf_op jit(solution)/shard_map/jit(dynamic_index_in_dim)/squeeze | solution.py:192
  26.2 2.3 convolution_convert_fusion.2
  28.5 4.9 %all-to-all-start.1 = ((bf16[8,96,1536]{2,1,0:T(8,128)(2,1)}), bf16[8,96,1536]{2,1,0:T(8,128)(2,1)}, u32[]{:S(2)}, u32[]{:S(2)}) async-start(bf16[8,96,1536]{2,1,0:T(8,128)(2,1)} %bitcast.7), calls=%async_computation.1 | async-start | bytes 4718592 | tf_op jit(solution)/shard_map/all_to_all | solution.py:208
  36.8 2.1 collective-permute-start
  38.9 32.2 %collective-permute-done.1.refs_1_ = bf16[512,1536]{1,0:T(8,128)(2,1)S(1)} collective-permute-done((bf16[512,1536]{1,0:T(8,128)(2,1)S(1)}, bf16[512,1536]{1,0:T(8,128)(2,1)S(1)}, u32[]{:S(2)}, u32[]{:S(2)}) %collective-permute-start.1) | collective-permute-done | bytes 1572896 | tf_op jit(solution)/shard_map/ppermute | solution.py:37
  73.6 3.0 %collective-permute-start.4 = (bf16[256,1536]{1,0:T(8,128)(2,1)S(1)}, bf16[256,1536]{1,0:T(8,128)(2,1)S(1)}, u32[]{:S(2)}, u32[]{:S(2)}) collective-permute-start(bf16[256,1536]{1,0:T(8,128)(2,1)S(1)} %slice.141), channel_id=1, source_target_pairs={{0,3},{1,0},{2,1},{3,2},{4,7},{5,4},{6,5},{7,6},{8,11},{9,8},{10,9... | collective-permute-start | bytes 2359304 | tf_op jit(solution)/shard_map/ppermute | solution.py:42
  76.6 5.2 %convolution_convert_fusion.4 = bf16[768,1536]{1,0:T(8,128)(2,1)} fusion(bf16[768,1536]{1,0:T(8,128)(2,1)} %bitcast.14, s32[768]{0:T(1024)S(1)} %fusion.29), kind=kOutput, calls=%fused_computation.4 | convolution fusion | flops 1813708800 | bytes 4721664 | tf_op jit(solution)/shard_map/dot_general | solution.py:15
  81.8 17.7 %collective-permute-done.refs_4_ = bf16[512,1536]{1,0:T(8,128)(2,1)} collective-permute-done((bf16[512,1536]{1,0:T(8,128)(2,1)}, bf16[512,1536]{1,0:T(8,128)(2,1)}, u32[]{:S(2)}, u32[]{:S(2)}) %collective-permute-start) | collective-permute-done | bytes 1572896 | tf_op jit(solution)/shard_map/ppermute | solution.py:196
  102.8 7.2 %convolution_convert_fusion.1 = bf16[768,2048]{1,0:T(8,128)(2,1)} fusion(bf16[1024,2048]{1,0:T(8,128)(2,1)} %all-gather.3.cloned.1.call-done, s32[1024]{0:T(1024)S(1)} %bitcast.56, s32[1024]{0:T(1024)S(1)} %bitcast.54, s32[1024]{0:T(1024)S(1)} %add_select_fusion.5, s32[768]{0:T(1024)S(1)} %get-tuple-element.86, s32[768]{0:T(1024)S(1)} %get-tuple-element.87), kind=kOutput, calls=%fused_computation.1 | convolution fusion | flops 3226730496 | bytes 7358464 | tf_op jit(solution)/shard_map/dot_general | solution.py:15
  110.0 4.8 %all-to-all-start.2 = ((bf16[8,96,2048]{2,1,0:T(8,128)(2,1)}), bf16[8,96,2048]{2,1,0:T(8,128)(2,1)S(1)}, u32[]{:S(2)}, u32[]{:S(2)}) async-start(bf16[8,96,2048]{2,1,0:T(8,128)(2,1)} %bitcast.47), calls=%async_computation.2 | async-start | bytes 6291456 | tf_op jit(solution)/shard_map/all_to_all | solution.py:225
  114.9 22.3 %collective-permute-done.5.refs_5_ = bf16[512,1536]{1,0:T(8,128)(2,1)} collective-permute-done((bf16[512,1536]{1,0:T(8,128)(2,1)}, bf16[512,1536]{1,0:T(8,128)(2,1)}, u32[]{:S(2)}, u32[]{:S(2)}) %collective-permute-start.5) | collective-permute-done | bytes 1572896 | tf_op jit(solution)/shard_map/ppermute | solution.py:37
  140.1 3.1 %collective-permute-start.8 = (bf16[256,1536]{1,0:T(8,128)(2,1)S(1)}, bf16[256,1536]{1,0:T(8,128)(2,1)}, u32[]{:S(2)}, u32[]{:S(2)}) collective-permute-start(bf16[256,1536]{1,0:T(8,128)(2,1)S(1)} %slice.143), channel_id=1, source_target_pairs={{0,3},{1,0},{2,1},{3,2},{4,7},{5,4},{6,5},{7,6},{8,11},{9,8},{10,9... | collective-permute-start | bytes 2359304 | tf_op jit(solution)/shard_map/ppermute | solution.py:42
  145.7 12.5 %collective-permute-done.6.refs_7_ = bf16[256,1536]{1,0:T(8,128)(2,1)S(1)} collective-permute-done((bf16[256,1536]{1,0:T(8,128)(2,1)S(1)}, bf16[256,1536]{1,0:T(8,128)(2,1)S(1)}, u32[]{:S(2)}, u32[]{:S(2)}) %collective-permute-start.6) | collective-permute-done | bytes 786464 | tf_op jit(solution)/shard_map/ppermute | solution.py:42
  159.7 7.2 %convolution_convert_fusion = bf16[768,2048]{1,0:T(8,128)(2,1)} fusion(bf16[1024,2048]{1,0:T(8,128)(2,1)} %all-gather.5.cloned.1.call-done, s32[1024]{0:T(1024)S(1)} %bitcast.57, s32[1024]{0:T(1024)S(1)} %bitcast.55, s32[1024]{0:T(1024)S(1)} %add_select_fusion.5, s32[768]{0:T(1024)S(1)} %get-tuple-element.86, s32[768]{0:T(1024)S(1)} %get-tuple-element.87), kind=kOutput, calls=%fused_computation | convolution fusion | flops 3226730496 | bytes 7358464 | tf_op jit(solution)/shard_map/dot_general | solution.py:15
  166.9 2.2 collective-permute-start.10
  170.7 5.1 %all-to-all-start.3 = ((bf16[8,96,2048]{2,1,0:T(8,128)(2,1)}), bf16[8,96,2048]{2,1,0:T(8,128)(2,1)}, u32[]{:S(2)}, u32[]{:S(2)}) async-start(bf16[8,96,2048]{2,1,0:T(8,128)(2,1)} %bitcast.48), calls=%async_computation.3 | async-start | bytes 6291456 | tf_op jit(solution)/shard_map/all_to_all | solution.py:225
  176.8 3.3 %collective-permute-start.11 = (bf16[96,1536]{1,0:T(8,128)(2,1)}, bf16[96,1536]{1,0:T(8,128)(2,1)S(1)}, u32[]{:S(2)}, u32[]{:S(2)}) collective-permute-start(bf16[96,1536]{1,0:T(8,128)(2,1)} %get-tuple-element.43), channel_id=1, source_target_pairs={{0,68},{4,128},{64,132},{68,192},{128,196},{132,0},{192,4},{196,64... | collective-permute-start | bytes 884744 | tf_op jit(solution)/shard_map/ppermute | solution.py:238
  180.1 2.7 collective-permute-start.12
  182.9 3.0 %collective-permute-start.13 = (bf16[96,1536]{1,0:T(8,128)(2,1)}, bf16[96,1536]{1,0:T(8,128)(2,1)S(1)}, u32[]{:S(2)}, u32[]{:S(2)}) collective-permute-start(bf16[96,1536]{1,0:T(8,128)(2,1)} %get-tuple-element.45), channel_id=1, source_target_pairs={{0,132},{4,192},{64,196},{68,0},{128,4},{132,64},{192,68},{196,128... | collective-permute-start | bytes 884744 | tf_op jit(solution)/shard_map/ppermute | solution.py:238
  185.9 3.4 %collective-permute-start.14 = (bf16[96,1536]{1,0:T(8,128)(2,1)}, bf16[96,1536]{1,0:T(8,128)(2,1)S(1)}, u32[]{:S(2)}, u32[]{:S(2)}) collective-permute-start(bf16[96,1536]{1,0:T(8,128)(2,1)} %get-tuple-element.46), channel_id=1, source_target_pairs={{0,192},{4,196},{64,0},{68,4},{128,64},{132,68},{192,128},{196,132... | collective-permute-start | bytes 884744 | tf_op jit(solution)/shard_map/ppermute | solution.py:238
  192.2 8.7 %collective-permute-done.11 = bf16[96,1536]{1,0:T(8,128)(2,1)S(1)} collective-permute-done((bf16[96,1536]{1,0:T(8,128)(2,1)}, bf16[96,1536]{1,0:T(8,128)(2,1)S(1)}, u32[]{:S(2)}, u32[]{:S(2)}) %collective-permute-start.11) | collective-permute-done | bytes 294944 | tf_op jit(solution)/shard_map/ppermute | solution.py:238
  200.9 9.0 %collective-permute-done.12 = bf16[96,1536]{1,0:T(8,128)(2,1)S(1)} collective-permute-done((bf16[96,1536]{1,0:T(8,128)(2,1)}, bf16[96,1536]{1,0:T(8,128)(2,1)S(1)}, u32[]{:S(2)}, u32[]{:S(2)}) %collective-permute-start.12) | collective-permute-done | bytes 294944 | tf_op jit(solution)/shard_map/ppermute | solution.py:238
  209.9 10.2 %collective-permute-done.13 = bf16[96,1536]{1,0:T(8,128)(2,1)S(1)} collective-permute-done((bf16[96,1536]{1,0:T(8,128)(2,1)}, bf16[96,1536]{1,0:T(8,128)(2,1)S(1)}, u32[]{:S(2)}, u32[]{:S(2)}) %collective-permute-start.13) | collective-permute-done | bytes 294944 | tf_op jit(solution)/shard_map/ppermute | solution.py:238
  220.1 10.9 %collective-permute-done.14 = bf16[96,1536]{1,0:T(8,128)(2,1)S(1)} collective-permute-done((bf16[96,1536]{1,0:T(8,128)(2,1)}, bf16[96,1536]{1,0:T(8,128)(2,1)S(1)}, u32[]{:S(2)}, u32[]{:S(2)}) %collective-permute-start.14) | collective-permute-done | bytes 294944 | tf_op jit(solution)/shard_map/ppermute | solution.py:238
  231.0 3.6 %collective-permute-done.15 = bf16[96,1536]{1,0:T(8,128)(2,1)S(1)} collective-permute-done((bf16[96,1536]{1,0:T(8,128)(2,1)}, bf16[96,1536]{1,0:T(8,128)(2,1)S(1)}, u32[]{:S(2)}, u32[]{:S(2)}) %collective-permute-start.15) | collective-permute-done | bytes 294944 | tf_op jit(solution)/shard_map/ppermute | solution.py:238
  234.7 3.6 %convolution_convert_fusion.3.g_ref = bf16[768,1536]{1,0:T(8,128)(2,1)} fusion(bf16[768,1536]{1,0:T(8,128)(2,1)S(1)} %constant_dynamic-update-slice_fusion, s32[768]{0:T(1024)S(1)} %fusion.28), kind=kOutput, calls=%fused_computation.3 | convolution fusion | flops 1813708800 | bytes 4721664 | tf_op jit(solution)/shard_map/dot_general | solution.py:15
  238.3 11.7 %half_products.1 = (f32[768,1536]{1,0:T(8,128)}, f32[768,16]{1,0:T(8,128)}) custom-call(s32[2]{0:T(128)} %pad_add_fusion.where_ref, bf16[768,2048]{1,0:T(8,128)(2,1)} %bitcast.45, bf16[16,2048]{1,0:T(8,128)(2,1)} %copy-done.10, bf16[512,1536]{1,0:T(8,128)(2,1)} %copy-done.3, bf16[512,1536]{1,0:T(8,128)(2,1)} %copy-done.4, ...), custom_call_target="tpu_custom_call" | custom-call | flops 4831838208 | bytes 14680064 | tf_op jit(solution)/shard_map/half_products/pallas_call | solution.py:118
  250.0 18.2 %gradients.1 = f32[4,16,1408]{2,1,0:T(8,128)} custom-call(s32[2]{0:T(128)} %pad_add_fusion.where_ref, bf16[768,2048]{1,0:T(8,128)(2,1)} %bitcast.46, bf16[768,2048]{1,0:T(8,128)(2,1)} %bitcast.18.xb_ref, bf16[768,1536]{1,0:T(8,128)(2,1)} %convolution_convert_fusion.3.g_ref, f32[768,1536]{1,0:T(8,128)} %get-tuple-element.50.frozen_ref, ...), custom_call_target="tpu_custom_call" | custom-call | tf_op jit(solution)/shard_map/gradients/pallas_call | solution.py:145
  268.2 11.9 %all_to_all.30 = f32[4,16,1408]{2,1,0:T(8,128)S(1)} all-to-all(f32[4,16,1408]{2,1,0:T(8,128)} %gradients.1), channel_id=1, replica_groups=mesh['zh'=4,'y'=4,'c'=2,'zl'=2,'x'=4] {'x'}, dimensions={0} | all-to-all | bytes 720896 | tf_op jit(solution)/shard_map/all_to_all | solution.py:262
  280.2 12.6 %all_to_all.31 = bf16[8,16,1408]{2,1,0:T(8,128)(2,1)S(1)} all-to-all(bf16[8,16,1408]{2,1,0:T(8,128)(2,1)S(1)} %broadcast_in_dim.5), channel_id=1, replica_groups=mesh['zh'=4,'y'=4,'c'=2,'zl'=2,'x'=4] {'zl','x'}, dimensions={0} | all-to-all | bytes 720896 | tf_op jit(solution)/shard_map/all_to_all | solution.py:265
  (90 shorter events, 28.4 us)
Async XLA Ops:
  7.2 29.6 %copy-start = (bf16[2,4096,16]{1,2,0:T(8,128)(2,1)S(1)}, bf16[2,4096,16]{1,2,0:T(8,128)(2,1)}, u32[]{:S(2)}) copy-start(bf16[2,4096,16]{1,2,0:T(8,128)(2,1)} %param.10) | copy-start | bytes 786436
  7.2 95.6 %all-gather.3.cloned.1.call-start = ((), (), s32[]{:S(2)}) async-start(), calls=%async_computation.6 | async-start | bytes 4718592 | tf_op jit(solution)/shard_map/all_gather | solution.py:185
  11.8 16.8 %all-to-all-start = ((s32[8,2,128]{2,1,0:T(2,128)}), s32[8,2,128]{2,1,0:T(2,128)S(1)}, u32[]{:S(2)}, u32[]{:S(2)}) async-start(s32[8,2,128]{2,1,0:T(2,128)} %broadcast_in_dim.4), calls=%async_computation | async-start | bytes 16384 | tf_op jit(solution)/shard_map/all_to_all | solution.py:190
  20.2 138.9 %all-gather.5.cloned.1.call-start = ((), (), s32[]{:S(2)}) async-start(), calls=%async_computation.7 | async-start | bytes 4718592 | tf_op jit(solution)/shard_map/all_gather | solution.py:185
  21.7 3.3 %copy-start.5 = (bf16[128,2,1536]{2,1,0:T(2,128)(2,1)S(1)}, bf16[128,2,1536]{2,1,0:T(2,128)(2,1)}, u32[]{:S(2)}) copy-start(bf16[128,2,1536]{2,1,0:T(2,128)(2,1)} %param.8) | copy-start | bytes 2359300
  25.0 9.9 %copy-start.3 = (bf16[512,1536]{1,0:T(8,128)(2,1)}, bf16[512,1536]{1,0:T(8,128)(2,1)S(1)}, u32[]{:S(2)}) copy-start(bf16[512,1536]{1,0:T(8,128)(2,1)S(1)} %get-tuple-element.54.refs_0_) | copy-start | bytes 4718596
  28.5 48.1 %all-to-all-start.1 = ((bf16[8,96,1536]{2,1,0:T(8,128)(2,1)}), bf16[8,96,1536]{2,1,0:T(8,128)(2,1)}, u32[]{:S(2)}, u32[]{:S(2)}) async-start(bf16[8,96,1536]{2,1,0:T(8,128)(2,1)} %bitcast.7), calls=%async_computation.1 | async-start | bytes 4718592 | tf_op jit(solution)/shard_map/all_to_all | solution.py:208
  33.5 37.6 %collective-permute-start.1 = (bf16[512,1536]{1,0:T(8,128)(2,1)S(1)}, bf16[512,1536]{1,0:T(8,128)(2,1)S(1)}, u32[]{:S(2)}, u32[]{:S(2)}) collective-permute-start(bf16[512,1536]{1,0:T(8,128)(2,1)S(1)} %get-tuple-element.54.refs_0_), channel_id=1, source_target_pairs={{0,1},{1,2},{2,3},{3,0},{4,5},{5,6},{6,7},{7,4},{8,9},{9,10},{10,1... | collective-permute-start | bytes 4718600 | tf_op jit(solution)/shard_map/ppermute | solution.py:37
  35.0 37.4 %collective-permute-start.3 = (bf16[512,1536]{1,0:T(8,128)(2,1)S(1)}, bf16[512,1536]{1,0:T(8,128)(2,1)}, u32[]{:S(2)}, u32[]{:S(2)}) collective-permute-start(bf16[512,1536]{1,0:T(8,128)(2,1)S(1)} %get-tuple-element.54.refs_0_), channel_id=1, source_target_pairs={{0,3},{1,0},{2,1},{3,2},{4,7},{5,4},{6,5},{7,6},{8,11},{9,8},{10,9... | collective-permute-start | bytes 4718600 | tf_op jit(solution)/shard_map/ppermute | solution.py:37
  36.8 62.7 %collective-permute-start = (bf16[512,1536]{1,0:T(8,128)(2,1)}, bf16[512,1536]{1,0:T(8,128)(2,1)}, u32[]{:S(2)}, u32[]{:S(2)}) collective-permute-start(bf16[512,1536]{1,0:T(8,128)(2,1)} %get-tuple-element.31), channel_id=1, source_target_pairs={{0,4},{4,0},{1,5},{5,1},{2,6},{6,2},{3,7},{7,3},{8,12},{12,8},{9,1... | collective-permute-start | bytes 4718600 | tf_op jit(solution)/shard_map/ppermute | solution.py:196
  71.1 10.7 %copy-start.4 = (bf16[512,1536]{1,0:T(8,128)(2,1)}, bf16[512,1536]{1,0:T(8,128)(2,1)S(1)}, u32[]{:S(2)}) copy-start(bf16[512,1536]{1,0:T(8,128)(2,1)S(1)} %collective-permute-done.1.refs_1_) | copy-start | bytes 4718596
  72.1 27.4 %collective-permute-start.2 = (bf16[256,1536]{1,0:T(8,128)(2,1)}, bf16[256,1536]{1,0:T(8,128)(2,1)}, u32[]{:S(2)}, u32[]{:S(2)}) collective-permute-start(bf16[256,1536]{1,0:T(8,128)(2,1)} %slice.140), channel_id=1, source_target_pairs={{0,1},{1,2},{2,3},{3,0},{4,5},{5,6},{6,7},{7,4},{8,9},{9,10},{10,1... | collective-permute-start | bytes 2359304 | tf_op jit(solution)/shard_map/ppermute | solution.py:42
  73.6 25.9 %collective-permute-start.4 = (bf16[256,1536]{1,0:T(8,128)(2,1)S(1)}, bf16[256,1536]{1,0:T(8,128)(2,1)S(1)}, u32[]{:S(2)}, u32[]{:S(2)}) collective-permute-start(bf16[256,1536]{1,0:T(8,128)(2,1)S(1)} %slice.141), channel_id=1, source_target_pairs={{0,3},{1,0},{2,1},{3,2},{4,7},{5,4},{6,5},{7,6},{8,11},{9,8},{10,9... | collective-permute-start | bytes 2359304 | tf_op jit(solution)/shard_map/ppermute | solution.py:42
  99.5 10.5 %copy-start.7 = (bf16[256,1536]{1,0:T(8,128)(2,1)}, bf16[256,1536]{1,0:T(8,128)(2,1)S(1)}, u32[]{:S(2)}) copy-start(bf16[256,1536]{1,0:T(8,128)(2,1)S(1)} %collective-permute-done.4.refs_3_) | copy-start | bytes 2359300
  99.5 37.7 %collective-permute-start.5 = (bf16[512,1536]{1,0:T(8,128)(2,1)}, bf16[512,1536]{1,0:T(8,128)(2,1)}, u32[]{:S(2)}, u32[]{:S(2)}) collective-permute-start(bf16[512,1536]{1,0:T(8,128)(2,1)} %collective-permute-done.refs_4_), channel_id=1, source_target_pairs={{0,1},{1,2},{2,3},{3,0},{4,5},{5,6},{6,7},{7,4},{8,9},{9,10},{10,1... | collective-permute-start | bytes 4718600 | tf_op jit(solution)/shard_map/ppermute | solution.py:37
  101.0 37.8 %collective-permute-start.7 = (bf16[512,1536]{1,0:T(8,128)(2,1)}, bf16[512,1536]{1,0:T(8,128)(2,1)}, u32[]{:S(2)}, u32[]{:S(2)}) collective-permute-start(bf16[512,1536]{1,0:T(8,128)(2,1)} %collective-permute-done.refs_4_), channel_id=1, source_target_pairs={{0,3},{1,0},{2,1},{3,2},{4,7},{5,4},{6,5},{7,6},{8,11},{9,8},{10,9... | collective-permute-start | bytes 4718600 | tf_op jit(solution)/shard_map/ppermute | solution.py:37
  110.0 59.1 %all-to-all-start.2 = ((bf16[8,96,2048]{2,1,0:T(8,128)(2,1)}), bf16[8,96,2048]{2,1,0:T(8,128)(2,1)S(1)}, u32[]{:S(2)}, u32[]{:S(2)}) async-start(bf16[8,96,2048]{2,1,0:T(8,128)(2,1)} %bitcast.47), calls=%async_computation.2 | async-start | bytes 6291456 | tf_op jit(solution)/shard_map/all_to_all | solution.py:225
  114.8 28.9 %copy-start.9 = (bf16[2,16,1536]{2,1,0:T(8,128)(2,1)S(1)}, bf16[2,16,1536]{2,1,0:T(8,128)(2,1)}, u32[]{:S(2)}) copy-start(bf16[2,16,1536]{2,1,0:T(8,128)(2,1)} %param.11) | copy-start | bytes 294916
  114.8 29.5 %copy-start.6 = (bf16[768,1536]{1,0:T(8,128)(2,1)S(1)}, bf16[768,1536]{1,0:T(8,128)(2,1)}, u32[]{:S(2)}) copy-start(bf16[768,1536]{1,0:T(8,128)(2,1)} %convolution_convert_fusion.4) | copy-start | bytes 7077892
  114.9 30.8 %copy-start.8 = (bf16[16,2048]{1,0:T(8,128)(2,1)}, bf16[16,2048]{1,0:T(8,128)(2,1)S(1)}, u32[]{:S(2)}) copy-start(bf16[16,2048]{1,0:T(8,128)(2,1)S(1)} %get-tuple-element.66.first_ref) | copy-start | bytes 196612
  114.9 30.8 %copy-start.10 = (bf16[16,2048]{1,0:T(8,128)(2,1)}, bf16[16,2048]{1,0:T(8,128)(2,1)S(1)}, u32[]{:S(2)}) copy-start(bf16[16,2048]{1,0:T(8,128)(2,1)S(1)} %get-tuple-element.67.first_ref) | copy-start | bytes 196612
  138.4 19.8 %collective-permute-start.6 = (bf16[256,1536]{1,0:T(8,128)(2,1)S(1)}, bf16[256,1536]{1,0:T(8,128)(2,1)S(1)}, u32[]{:S(2)}, u32[]{:S(2)}) collective-permute-start(bf16[256,1536]{1,0:T(8,128)(2,1)S(1)} %slice.142), channel_id=1, source_target_pairs={{0,1},{1,2},{2,3},{3,0},{4,5},{5,6},{6,7},{7,4},{8,9},{9,10},{10,1... | collective-permute-start | bytes 2359304 | tf_op jit(solution)/shard_map/ppermute | solution.py:42
  140.1 19.0 %collective-permute-start.8 = (bf16[256,1536]{1,0:T(8,128)(2,1)S(1)}, bf16[256,1536]{1,0:T(8,128)(2,1)}, u32[]{:S(2)}, u32[]{:S(2)}) collective-permute-start(bf16[256,1536]{1,0:T(8,128)(2,1)S(1)} %slice.143), channel_id=1, source_target_pairs={{0,3},{1,0},{2,1},{3,2},{4,7},{5,4},{6,5},{7,6},{8,11},{9,8},{10,9... | collective-permute-start | bytes 2359304 | tf_op jit(solution)/shard_map/ppermute | solution.py:42
  159.1 26.8 %collective-permute-start.9 = (bf16[96,1536]{1,0:T(8,128)(2,1)}, bf16[96,1536]{1,0:T(8,128)(2,1)}, u32[]{:S(2)}, u32[]{:S(2)}) collective-permute-start(bf16[96,1536]{1,0:T(8,128)(2,1)} %get-tuple-element.41), channel_id=1, source_target_pairs={{0,4},{4,64},{64,68},{68,128},{128,132},{132,192},{192,196},{196,0... | collective-permute-start | bytes 884744 | tf_op jit(solution)/shard_map/ppermute | solution.py:238
  166.9 23.4 %collective-permute-start.10 = (bf16[96,1536]{1,0:T(8,128)(2,1)}, bf16[96,1536]{1,0:T(8,128)(2,1)}, u32[]{:S(2)}, u32[]{:S(2)}) collective-permute-start(bf16[96,1536]{1,0:T(8,128)(2,1)} %get-tuple-element.42), channel_id=1, source_target_pairs={{0,64},{4,68},{64,128},{68,132},{128,192},{132,196},{192,0},{196,4... | collective-permute-start | bytes 884744 | tf_op jit(solution)/shard_map/ppermute | solution.py:238
  170.7 79.2 %all-to-all-start.3 = ((bf16[8,96,2048]{2,1,0:T(8,128)(2,1)}), bf16[8,96,2048]{2,1,0:T(8,128)(2,1)}, u32[]{:S(2)}, u32[]{:S(2)}) async-start(bf16[8,96,2048]{2,1,0:T(8,128)(2,1)} %bitcast.48), calls=%async_computation.3 | async-start | bytes 6291456 | tf_op jit(solution)/shard_map/all_to_all | solution.py:225
  176.8 24.0 %collective-permute-start.11 = (bf16[96,1536]{1,0:T(8,128)(2,1)}, bf16[96,1536]{1,0:T(8,128)(2,1)S(1)}, u32[]{:S(2)}, u32[]{:S(2)}) collective-permute-start(bf16[96,1536]{1,0:T(8,128)(2,1)} %get-tuple-element.43), channel_id=1, source_target_pairs={{0,68},{4,128},{64,132},{68,192},{128,196},{132,0},{192,4},{196,64... | collective-permute-start | bytes 884744 | tf_op jit(solution)/shard_map/ppermute | solution.py:238
  180.1 29.7 %collective-permute-start.12 = (bf16[96,1536]{1,0:T(8,128)(2,1)}, bf16[96,1536]{1,0:T(8,128)(2,1)S(1)}, u32[]{:S(2)}, u32[]{:S(2)}) collective-permute-start(bf16[96,1536]{1,0:T(8,128)(2,1)} %get-tuple-element.44), channel_id=1, source_target_pairs={{0,128},{4,132},{64,192},{68,196},{128,0},{132,4},{192,64},{196,68... | collective-permute-start | bytes 884744 | tf_op jit(solution)/shard_map/ppermute | solution.py:238
  182.9 37.2 %collective-permute-start.13 = (bf16[96,1536]{1,0:T(8,128)(2,1)}, bf16[96,1536]{1,0:T(8,128)(2,1)S(1)}, u32[]{:S(2)}, u32[]{:S(2)}) collective-permute-start(bf16[96,1536]{1,0:T(8,128)(2,1)} %get-tuple-element.45), channel_id=1, source_target_pairs={{0,132},{4,192},{64,196},{68,0},{128,4},{132,64},{192,68},{196,128... | collective-permute-start | bytes 884744 | tf_op jit(solution)/shard_map/ppermute | solution.py:238
  185.9 45.1 %collective-permute-start.14 = (bf16[96,1536]{1,0:T(8,128)(2,1)}, bf16[96,1536]{1,0:T(8,128)(2,1)S(1)}, u32[]{:S(2)}, u32[]{:S(2)}) collective-permute-start(bf16[96,1536]{1,0:T(8,128)(2,1)} %get-tuple-element.46), channel_id=1, source_target_pairs={{0,192},{4,196},{64,0},{68,4},{128,64},{132,68},{192,128},{196,132... | collective-permute-start | bytes 884744 | tf_op jit(solution)/shard_map/ppermute | solution.py:238
  190.3 44.4 %collective-permute-start.15 = (bf16[96,1536]{1,0:T(8,128)(2,1)}, bf16[96,1536]{1,0:T(8,128)(2,1)S(1)}, u32[]{:S(2)}, u32[]{:S(2)}) collective-permute-start(bf16[96,1536]{1,0:T(8,128)(2,1)} %get-tuple-element.47), channel_id=1, source_target_pairs={{0,196},{4,0},{64,4},{68,64},{128,68},{132,128},{192,132},{196,192... | collective-permute-start | bytes 884744 | tf_op jit(solution)/shard_map/ppermute | solution.py:238
  250.0 44.4 %copy-start.1 = (bf16[2,4096,16]{1,2,0:T(8,128)(2,1)S(1)}, bf16[2,4096,16]{1,2,0:T(8,128)(2,1)}, u32[]{:S(2)}) copy-start(bf16[2,4096,16]{1,2,0:T(8,128)(2,1)} %param.10) | copy-start | bytes 786436
  (2 other events, 2.5 us)
Sparse Core Ops, SparseCore 0:
  10.3 81.8 all-gather.2
  94.1 56.1 all-gather.4
where the time goes:
time: 302 us; the launch traced here: 301 us
  waiting for transfers between devices  128 us (42%)
  starting transfers between devices  55.2 us (18%)
  Pallas kernels  32.2 us (11%)
  matrix products  25.4 us (8%)
  blocking collectives  24.6 us (8%)
  local copies, waits for them, and re-layouts  17.5 us (6%)
  between operations  14.3 us (5%)
  other arithmetic  4.5 us (1%)
    ppermute x4, waiting for transfers between devices, first_hop(): return (lax.ppermute(shard, 'x', RIGHT), lax.ppermute(shard, 'x', LEFT))  54.4 us
    ppermute x7, waiting for transfers between devices, local(): blocks_g[n] = lax.ppermute(blocks_g[n], ('zh', 'zl'), moves)  42.4 us
    dot_general x5, matrix products, dot(): lax.dot_general(a, b, (dims, ((), ())), preferred_element_type=jnp.float32)  25.4 us
    pallas_call x1, Pallas kernels, gradients(): pl.pallas_call(final_kernel, grid_spec=pltpu.PrefetchScalarGridSpec(num_s...  18.2 us
    ppermute x1, waiting for transfers between devices, local(): got = lax.ppermute(other, 'zl', [(0, 1), (1, 0)])  17.7 us
    ppermute x7, starting transfers between devices, local(): blocks_g[n] = lax.ppermute(blocks_g[n], ('zh', 'zl'), moves)  16.2 us
    all_to_all x1, blocking collectives, local(): lax.all_to_all(total, DP_AXES, split_axis=0, concat_axis=0, tiled=True)  12.6 us
    ppermute x2, waiting for transfers between devices, second_hop(): lax.ppermute(before[:half], 'x', RIGHT)  12.5 us
  transfers between devices with their start and end apart: 22, of which 9 were waited for; matrix products, arithmetic and copies ran while one was open for 14% of the time, Pallas kernels for 4%

commit v1 on v0

--- a/solution.py
+++ b/solution.py
@@ -95,6 +95,8 @@
 
 
 ROW_BLOCK = 256
+EARLY = (4,)
+LATE = (5, 3, 6, 7, 1)
 
 
 def row_spec(array):
@@ -228,20 +230,27 @@
     near_opposite = second_hop(*near)
     got, near_opposite, column_g = lax.optimization_barrier((got, near_opposite, column_g))
     far = first_hop(got)
-    line0, near_opposite = lax.optimization_barrier((lines[0], near_opposite))
+    line0, near_opposite, column_g = lax.optimization_barrier((lines[0], near_opposite, column_g))
     xa = spread(packed(line0))
+    blocks_g = [column_g[n * depth * cap : (n + 1) * depth * cap] for n in range(depth)]
+
+    def pass_ahead(n):
+        moves = [(i, (i + n) % depth) for i in range(depth)]
+        return lax.ppermute(blocks_g[n], ("zh", "zl"), moves)
+
+    two_ahead = pass_ahead(2)
     far_opposite = second_hop(*far)
-    blocks_g = [column_g[n * depth * cap : (n + 1) * depth * cap] for n in range(depth)]
     line1, far_opposite, blocks_g = lax.optimization_barrier((lines[1], far_opposite, blocks_g))
-    for n in (4, 5, 3, 6, 2, 7, 1):
-        moves = [(i, (i + n) % depth) for i in range(depth)]
-        blocks_g[n] = lax.ppermute(blocks_g[n], ("zh", "zl"), moves)
+    for n in EARLY + LATE:
+        blocks_g[n] = pass_ahead(n)
+    blocks_g[2] = two_ahead
     xb = spread(packed(line1))
 
     behind = (zi - inner) % depth
-    order = (behind * depth + outer) * cap + rank
+    stand = jnp.where(behind < 3, behind, jnp.where(behind == 3, 7, jnp.where(behind == 4, 6, behind - 2)))
+    order = (stand * depth + outer) * cap + rank
     order = (order[:, None] == row[None, :]).astype(jnp.bfloat16)
-    rows_g = dot(order, jnp.concatenate(blocks_g, axis=0)).astype(jnp.bfloat16)
+    rows_g = dot(order, jnp.concatenate([blocks_g[n] for n in (0, 1, 2, 5, 6, 7, 4, 3)], axis=0)).astype(jnp.bfloat16)
 
     first = lax.dynamic_index_in_dim(adapter_first, zl, 0, keepdims=False)
     second = lax.dynamic_index_in_dim(adapter_second, zl, 0, keepdims=False)

time: 302 us -> 298 us (0.987)
  waiting for transfers between devices: 128 us -> 115 us
  blocking collectives: 24.6 us -> 35 us
    ppermute x7, waiting for transfers between devices: 42.4 us -> 31.8 us  [pass_ahead(): return lax.ppermute(blocks_g[n], ('zh', 'zl'), moves)]
    all_to_all x1, blocking collectives: 12.6 us -> 22.3 us  [local(): lax.all_to_all(total, DP_AXES, split_axis=0, concat_axis=0, tiled=True)]
  transfers between devices with their start and end apart: 22 -> 22, of which waited for: 9 -> 8; matrix products, arithmetic and copies ran while one was open for 14% -> 15% of each run, Pallas kernels for 4% -> 4%
where the time goes in v1:
time: 298 us; the launch traced here: 297 us
  waiting for transfers between devices  115 us (39%)
  starting transfers between devices  53.5 us (18%)
  blocking collectives  35 us (12%)
  Pallas kernels  32.2 us (11%)
  matrix products  25.4 us (9%)
  local copies, waits for them, and re-layouts  17.5 us (6%)
  between operations  14.3 us (5%)
  other arithmetic  4.51 us (2%)
    ppermute x4, waiting for transfers between devices, first_hop(): return (lax.ppermute(shard, 'x', RIGHT), lax.ppermute(shard, 'x', LEFT))  54.4 us
    ppermute x7, waiting for transfers between devices, pass_ahead(): return lax.ppermute(blocks_g[n], ('zh', 'zl'), moves)  31.8 us
    dot_general x5, matrix products, dot(): lax.dot_general(a, b, (dims, ((), ())), preferred_element_type=jnp.float32)  25.4 us
    all_to_all x1, blocking collectives, local(): lax.all_to_all(total, DP_AXES, split_axis=0, concat_axis=0, tiled=True)  22.3 us
    pallas_call x1, Pallas kernels, gradients(): pl.pallas_call(final_kernel, grid_spec=pltpu.PrefetchScalarGridSpec(num_s...  18.2 us
    ppermute x1, waiting for transfers between devices, local(): got = lax.ppermute(other, 'zl', [(0, 1), (1, 0)])  17.7 us
    ppermute x7, starting transfers between devices, pass_ahead(): return lax.ppermute(blocks_g[n], ('zh', 'zl'), moves)  14.6 us
    all_to_all x1, blocking collectives, local(): parts = lax.all_to_all(parts, 'x', split_axis=0, concat_axis=0, tiled=True)  12.6 us
  transfers between devices with their start and end apart: 22, of which 8 were waited for; matrix products, arithmetic and copies ran while one was open for 15% of the time, Pallas kernels for 4%

profile of v1, /device:TPU:8, one launch (start us, length us, event | category | flops | bytes accessed | tf_op | source)
XLA Modules:
  0.0 296.9 jit_solution(3576030185338953505)
XLA Ops:
  7.2 2.3 split_columns.1
  11.8 8.5 %all-to-all-start = ((s32[8,2,128]{2,1,0:T(2,128)}), s32[8,2,128]{2,1,0:T(2,128)S(1)}, u32[]{:S(2)}, u32[]{:S(2)}) async-start(s32[8,2,128]{2,1,0:T(2,128)} %broadcast_in_dim.8), calls=%async_computation | async-start | bytes 16384 | tf_op jit(solution)/shard_map/all_to_all | solution.py:192
  21.7 3.3 %dynamic-slice_bitcast_fusion = (bf16[512,1536]{1,0:T(8,128)(2,1)S(1)}, bf16[512,1536]{1,0:T(8,128)(2,1)}) fusion(bf16[2,512,1536]{2,1,0:T(8,128)(2,1)} %param.9, s32[]{:T(128)S(6)} %select_n.182, s32[]{:T(128)S(6)} %select_n.181), kind=kLoop, calls=%fused_computation.8 | loop fusion | bytes 6291464 | tf_op jit(solution)/shard_map/jit(dynamic_index_in_dim)/squeeze | solution.py:194
  26.2 2.3 convolution_convert_fusion.2
  28.5 4.9 %all-to-all-start.1 = ((bf16[8,96,1536]{2,1,0:T(8,128)(2,1)}), bf16[8,96,1536]{2,1,0:T(8,128)(2,1)}, u32[]{:S(2)}, u32[]{:S(2)}) async-start(bf16[8,96,1536]{2,1,0:T(8,128)(2,1)} %bitcast.7), calls=%async_computation.1 | async-start | bytes 4718592 | tf_op jit(solution)/shard_map/all_to_all | solution.py:210
  35.0 1.7 collective-permute-start.3
  36.8 2.1 collective-permute-start
  38.9 32.2 %collective-permute-done.1.refs_1_ = bf16[512,1536]{1,0:T(8,128)(2,1)S(1)} collective-permute-done((bf16[512,1536]{1,0:T(8,128)(2,1)S(1)}, bf16[512,1536]{1,0:T(8,128)(2,1)S(1)}, u32[]{:S(2)}, u32[]{:S(2)}) %collective-permute-start.1) | collective-permute-done | bytes 1572896 | tf_op jit(solution)/shard_map/ppermute | solution.py:37
  73.6 3.0 %collective-permute-start.4 = (bf16[256,1536]{1,0:T(8,128)(2,1)S(1)}, bf16[256,1536]{1,0:T(8,128)(2,1)S(1)}, u32[]{:S(2)}, u32[]{:S(2)}) collective-permute-start(bf16[256,1536]{1,0:T(8,128)(2,1)S(1)} %slice.141), channel_id=1, source_target_pairs={{0,3},{1,0},{2,1},{3,2},{4,7},{5,4},{6,5},{7,6},{8,11},{9,8},{10,9... | collective-permute-start | bytes 2359304 | tf_op jit(solution)/shard_map/ppermute | solution.py:42
  76.6 5.2 %convolution_convert_fusion.4 = bf16[768,1536]{1,0:T(8,128)(2,1)} fusion(bf16[768,1536]{1,0:T(8,128)(2,1)} %bitcast.14, s32[768]{0:T(1024)S(1)} %fusion.26), kind=kOutput, calls=%fused_computation.4 | convolution fusion | flops 1813708800 | bytes 4721664 | tf_op jit(solution)/shard_map/dot_general | solution.py:15
  81.8 17.7 %collective-permute-done.refs_4_ = bf16[512,1536]{1,0:T(8,128)(2,1)} collective-permute-done((bf16[512,1536]{1,0:T(8,128)(2,1)}, bf16[512,1536]{1,0:T(8,128)(2,1)}, u32[]{:S(2)}, u32[]{:S(2)}) %collective-permute-start) | collective-permute-done | bytes 1572896 | tf_op jit(solution)/shard_map/ppermute | solution.py:198
  101.0 1.8 collective-permute-start.7
  102.8 7.2 %convolution_convert_fusion.1 = bf16[768,2048]{1,0:T(8,128)(2,1)} fusion(bf16[1024,2048]{1,0:T(8,128)(2,1)} %all-gather.3.cloned.1.call-done, s32[1024]{0:T(1024)S(1)} %bitcast.56, s32[1024]{0:T(1024)S(1)} %bitcast.54, s32[1024]{0:T(1024)S(1)} %add_select_fusion.5, s32[768]{0:T(1024)S(1)} %get-tuple-element.86, s32[768]{0:T(1024)S(1)} %get-tuple-element.87), kind=kOutput, calls=%fused_computation.1 | convolution fusion | flops 3226730496 | bytes 7358464 | tf_op jit(solution)/shard_map/dot_general | solution.py:15
  110.0 4.8 %all-to-all-start.2 = ((bf16[8,96,2048]{2,1,0:T(8,128)(2,1)}), bf16[8,96,2048]{2,1,0:T(8,128)(2,1)S(1)}, u32[]{:S(2)}, u32[]{:S(2)}) async-start(bf16[8,96,2048]{2,1,0:T(8,128)(2,1)} %bitcast.47), calls=%async_computation.2 | async-start | bytes 6291456 | tf_op jit(solution)/shard_map/all_to_all | solution.py:227
  114.9 22.3 %collective-permute-done.5.refs_5_ = bf16[512,1536]{1,0:T(8,128)(2,1)} collective-permute-done((bf16[512,1536]{1,0:T(8,128)(2,1)}, bf16[512,1536]{1,0:T(8,128)(2,1)}, u32[]{:S(2)}, u32[]{:S(2)}) %collective-permute-start.5) | collective-permute-done | bytes 1572896 | tf_op jit(solution)/shard_map/ppermute | solution.py:37
  140.1 3.1 %collective-permute-start.8 = (bf16[256,1536]{1,0:T(8,128)(2,1)S(1)}, bf16[256,1536]{1,0:T(8,128)(2,1)}, u32[]{:S(2)}, u32[]{:S(2)}) collective-permute-start(bf16[256,1536]{1,0:T(8,128)(2,1)S(1)} %slice.143), channel_id=1, source_target_pairs={{0,3},{1,0},{2,1},{3,2},{4,7},{5,4},{6,5},{7,6},{8,11},{9,8},{10,9... | collective-permute-start | bytes 2359304 | tf_op jit(solution)/shard_map/ppermute | solution.py:42
  145.7 2.5 collective-permute-start.10
  148.2 10.0 %collective-permute-done.6.refs_7_ = bf16[256,1536]{1,0:T(8,128)(2,1)S(1)} collective-permute-done((bf16[256,1536]{1,0:T(8,128)(2,1)S(1)}, bf16[256,1536]{1,0:T(8,128)(2,1)S(1)}, u32[]{:S(2)}, u32[]{:S(2)}) %collective-permute-start.6) | collective-permute-done | bytes 786464 | tf_op jit(solution)/shard_map/ppermute | solution.py:42
  159.7 7.2 %convolution_convert_fusion = bf16[768,2048]{1,0:T(8,128)(2,1)} fusion(bf16[1024,2048]{1,0:T(8,128)(2,1)} %all-gather.5.cloned.1.call-done, s32[1024]{0:T(1024)S(1)} %bitcast.57, s32[1024]{0:T(1024)S(1)} %bitcast.55, s32[1024]{0:T(1024)S(1)} %add_select_fusion.5, s32[768]{0:T(1024)S(1)} %get-tuple-element.86, s32[768]{0:T(1024)S(1)} %get-tuple-element.87), kind=kOutput, calls=%fused_computation | convolution fusion | flops 3226730496 | bytes 7358464 | tf_op jit(solution)/shard_map/dot_general | solution.py:15
  167.0 1.6 copy-done.2
  168.6 5.1 %all-to-all-start.3 = ((bf16[8,96,2048]{2,1,0:T(8,128)(2,1)}), bf16[8,96,2048]{2,1,0:T(8,128)(2,1)}, u32[]{:S(2)}, u32[]{:S(2)}) async-start(bf16[8,96,2048]{2,1,0:T(8,128)(2,1)} %bitcast.48), calls=%async_computation.3 | async-start | bytes 6291456 | tf_op jit(solution)/shard_map/all_to_all | solution.py:227
  174.7 4.1 %collective-permute-start.11 = (bf16[96,1536]{1,0:T(8,128)(2,1)}, bf16[96,1536]{1,0:T(8,128)(2,1)S(1)}, u32[]{:S(2)}, u32[]{:S(2)}) collective-permute-start(bf16[96,1536]{1,0:T(8,128)(2,1)} %get-tuple-element.43), channel_id=1, source_target_pairs={{0,132},{4,192},{64,196},{68,0},{128,4},{132,64},{192,68},{196,128... | collective-permute-start | bytes 884744 | tf_op jit(solution)/shard_map/ppermute | solution.py:239
  178.7 3.3 %collective-permute-start.12 = (bf16[96,1536]{1,0:T(8,128)(2,1)}, bf16[96,1536]{1,0:T(8,128)(2,1)S(1)}, u32[]{:S(2)}, u32[]{:S(2)}) collective-permute-start(bf16[96,1536]{1,0:T(8,128)(2,1)} %get-tuple-element.44), channel_id=1, source_target_pairs={{0,192},{4,196},{64,0},{68,4},{128,64},{132,68},{192,128},{196,132... | collective-permute-start | bytes 884744 | tf_op jit(solution)/shard_map/ppermute | solution.py:239
  182.0 3.0 %collective-permute-start.14 = (bf16[96,1536]{1,0:T(8,128)(2,1)}, bf16[96,1536]{1,0:T(8,128)(2,1)S(1)}, u32[]{:S(2)}, u32[]{:S(2)}) collective-permute-start(bf16[96,1536]{1,0:T(8,128)(2,1)} %get-tuple-element.46), channel_id=1, source_target_pairs={{0,128},{4,132},{64,192},{68,196},{128,0},{132,4},{192,64},{196,68... | collective-permute-start | bytes 884744 | tf_op jit(solution)/shard_map/ppermute | solution.py:239
  188.1 15.0 %collective-permute-done.11 = bf16[96,1536]{1,0:T(8,128)(2,1)S(1)} collective-permute-done((bf16[96,1536]{1,0:T(8,128)(2,1)}, bf16[96,1536]{1,0:T(8,128)(2,1)S(1)}, u32[]{:S(2)}, u32[]{:S(2)}) %collective-permute-start.11) | collective-permute-done | bytes 294944 | tf_op jit(solution)/shard_map/ppermute | solution.py:239
  203.1 9.2 %collective-permute-done.12 = bf16[96,1536]{1,0:T(8,128)(2,1)S(1)} collective-permute-done((bf16[96,1536]{1,0:T(8,128)(2,1)}, bf16[96,1536]{1,0:T(8,128)(2,1)S(1)}, u32[]{:S(2)}, u32[]{:S(2)}) %collective-permute-start.12) | collective-permute-done | bytes 294944 | tf_op jit(solution)/shard_map/ppermute | solution.py:239
  212.4 6.7 %collective-permute-done.13 = bf16[96,1536]{1,0:T(8,128)(2,1)S(1)} collective-permute-done((bf16[96,1536]{1,0:T(8,128)(2,1)}, bf16[96,1536]{1,0:T(8,128)(2,1)S(1)}, u32[]{:S(2)}, u32[]{:S(2)}) %collective-permute-start.13) | collective-permute-done | bytes 294944 | tf_op jit(solution)/shard_map/ppermute | solution.py:239
  220.1 3.5 %convolution_convert_fusion.3.g_ref = bf16[768,1536]{1,0:T(8,128)(2,1)} fusion(bf16[768,1536]{1,0:T(8,128)(2,1)S(1)} %constant_dynamic-update-slice_fusion, s32[768]{0:T(1024)S(1)} %fusion.25), kind=kOutput, calls=%fused_computation.3 | convolution fusion | flops 1813708800 | bytes 4721664 | tf_op jit(solution)/shard_map/dot_general | solution.py:15
  223.6 11.7 %half_products.1 = (f32[768,1536]{1,0:T(8,128)}, f32[768,16]{1,0:T(8,128)}) custom-call(s32[2]{0:T(128)} %pad_add_fusion.where_ref, bf16[768,2048]{1,0:T(8,128)(2,1)} %bitcast.45, bf16[16,2048]{1,0:T(8,128)(2,1)} %copy-done.10, bf16[512,1536]{1,0:T(8,128)(2,1)} %copy-done.3, bf16[512,1536]{1,0:T(8,128)(2,1)} %copy-done.4, ...), custom_call_target="tpu_custom_call" | custom-call | flops 4831838208 | bytes 14680064 | tf_op jit(solution)/shard_map/half_products/pallas_call | solution.py:120
  235.3 18.2 %gradients.1 = f32[4,16,1408]{2,1,0:T(8,128)} custom-call(s32[2]{0:T(128)} %pad_add_fusion.where_ref, bf16[768,2048]{1,0:T(8,128)(2,1)} %bitcast.46, bf16[768,2048]{1,0:T(8,128)(2,1)} %bitcast.18.xb_ref, bf16[768,1536]{1,0:T(8,128)(2,1)} %convolution_convert_fusion.3.g_ref, f32[768,1536]{1,0:T(8,128)} %get-tuple-element.50.frozen_ref, ...), custom_call_target="tpu_custom_call" | custom-call | tf_op jit(solution)/shard_map/gradients/pallas_call | solution.py:147
  253.5 12.6 %all_to_all.30 = f32[4,16,1408]{2,1,0:T(8,128)S(1)} all-to-all(f32[4,16,1408]{2,1,0:T(8,128)} %gradients.1), channel_id=1, replica_groups=mesh['zh'=4,'y'=4,'c'=2,'zl'=2,'x'=4] {'x'}, dimensions={0} | all-to-all | bytes 720896 | tf_op jit(solution)/shard_map/all_to_all | solution.py:271
  266.2 22.3 %all_to_all.31 = bf16[8,16,1408]{2,1,0:T(8,128)(2,1)S(1)} all-to-all(bf16[8,16,1408]{2,1,0:T(8,128)(2,1)S(1)} %broadcast_in_dim.10), channel_id=1, replica_groups=mesh['zh'=4,'y'=4,'c'=2,'zl'=2,'x'=4] {'zl','x'}, dimensions={0} | all-to-all | bytes 720896 | tf_op jit(solution)/shard_map/all_to_all | solution.py:274
  (90 shorter events, 24.3 us)
Async XLA Ops:
  7.2 29.6 %copy-start = (bf16[2,4096,16]{1,2,0:T(8,128)(2,1)S(1)}, bf16[2,4096,16]{1,2,0:T(8,128)(2,1)}, u32[]{:S(2)}) copy-start(bf16[2,4096,16]{1,2,0:T(8,128)(2,1)} %param.10) | copy-start | bytes 786436
  7.2 95.6 %all-gather.3.cloned.1.call-start = ((), (), s32[]{:S(2)}) async-start(), calls=%async_computation.6 | async-start | bytes 4718592 | tf_op jit(solution)/shard_map/all_gather | solution.py:187
  11.8 16.8 %all-to-all-start = ((s32[8,2,128]{2,1,0:T(2,128)}), s32[8,2,128]{2,1,0:T(2,128)S(1)}, u32[]{:S(2)}, u32[]{:S(2)}) async-start(s32[8,2,128]{2,1,0:T(2,128)} %broadcast_in_dim.8), calls=%async_computation | async-start | bytes 16384 | tf_op jit(solution)/shard_map/all_to_all | solution.py:192
  20.2 138.9 %all-gather.5.cloned.1.call-start = ((), (), s32[]{:S(2)}) async-start(), calls=%async_computation.7 | async-start | bytes 4718592 | tf_op jit(solution)/shard_map/all_gather | solution.py:187
  21.7 3.3 %copy-start.5 = (bf16[128,2,1536]{2,1,0:T(2,128)(2,1)S(1)}, bf16[128,2,1536]{2,1,0:T(2,128)(2,1)}, u32[]{:S(2)}) copy-start(bf16[128,2,1536]{2,1,0:T(2,128)(2,1)} %param.8) | copy-start | bytes 2359300
  25.0 9.9 %copy-start.3 = (bf16[512,1536]{1,0:T(8,128)(2,1)}, bf16[512,1536]{1,0:T(8,128)(2,1)S(1)}, u32[]{:S(2)}) copy-start(bf16[512,1536]{1,0:T(8,128)(2,1)S(1)} %get-tuple-element.54.refs_0_) | copy-start | bytes 4718596
  28.5 48.1 %all-to-all-start.1 = ((bf16[8,96,1536]{2,1,0:T(8,128)(2,1)}), bf16[8,96,1536]{2,1,0:T(8,128)(2,1)}, u32[]{:S(2)}, u32[]{:S(2)}) async-start(bf16[8,96,1536]{2,1,0:T(8,128)(2,1)} %bitcast.7), calls=%async_computation.1 | async-start | bytes 4718592 | tf_op jit(solution)/shard_map/all_to_all | solution.py:210
  33.5 37.6 %collective-permute-start.1 = (bf16[512,1536]{1,0:T(8,128)(2,1)S(1)}, bf16[512,1536]{1,0:T(8,128)(2,1)S(1)}, u32[]{:S(2)}, u32[]{:S(2)}) collective-permute-start(bf16[512,1536]{1,0:T(8,128)(2,1)S(1)} %get-tuple-element.54.refs_0_), channel_id=1, source_target_pairs={{0,1},{1,2},{2,3},{3,0},{4,5},{5,6},{6,7},{7,4},{8,9},{9,10},{10,1... | collective-permute-start | bytes 4718600 | tf_op jit(solution)/shard_map/ppermute | solution.py:37
  35.0 37.4 %collective-permute-start.3 = (bf16[512,1536]{1,0:T(8,128)(2,1)S(1)}, bf16[512,1536]{1,0:T(8,128)(2,1)}, u32[]{:S(2)}, u32[]{:S(2)}) collective-permute-start(bf16[512,1536]{1,0:T(8,128)(2,1)S(1)} %get-tuple-element.54.refs_0_), channel_id=1, source_target_pairs={{0,3},{1,0},{2,1},{3,2},{4,7},{5,4},{6,5},{7,6},{8,11},{9,8},{10,9... | collective-permute-start | bytes 4718600 | tf_op jit(solution)/shard_map/ppermute | solution.py:37
  36.8 62.7 %collective-permute-start = (bf16[512,1536]{1,0:T(8,128)(2,1)}, bf16[512,1536]{1,0:T(8,128)(2,1)}, u32[]{:S(2)}, u32[]{:S(2)}) collective-permute-start(bf16[512,1536]{1,0:T(8,128)(2,1)} %get-tuple-element.31), channel_id=1, source_target_pairs={{0,4},{4,0},{1,5},{5,1},{2,6},{6,2},{3,7},{7,3},{8,12},{12,8},{9,1... | collective-permute-start | bytes 4718600 | tf_op jit(solution)/shard_map/ppermute | solution.py:198
  71.1 10.7 %copy-start.4 = (bf16[512,1536]{1,0:T(8,128)(2,1)}, bf16[512,1536]{1,0:T(8,128)(2,1)S(1)}, u32[]{:S(2)}) copy-start(bf16[512,1536]{1,0:T(8,128)(2,1)S(1)} %collective-permute-done.1.refs_1_) | copy-start | bytes 4718596
  72.1 27.4 %collective-permute-start.2 = (bf16[256,1536]{1,0:T(8,128)(2,1)}, bf16[256,1536]{1,0:T(8,128)(2,1)}, u32[]{:S(2)}, u32[]{:S(2)}) collective-permute-start(bf16[256,1536]{1,0:T(8,128)(2,1)} %slice.140), channel_id=1, source_target_pairs={{0,1},{1,2},{2,3},{3,0},{4,5},{5,6},{6,7},{7,4},{8,9},{9,10},{10,1... | collective-permute-start | bytes 2359304 | tf_op jit(solution)/shard_map/ppermute | solution.py:42
  73.6 25.9 %collective-permute-start.4 = (bf16[256,1536]{1,0:T(8,128)(2,1)S(1)}, bf16[256,1536]{1,0:T(8,128)(2,1)S(1)}, u32[]{:S(2)}, u32[]{:S(2)}) collective-permute-start(bf16[256,1536]{1,0:T(8,128)(2,1)S(1)} %slice.141), channel_id=1, source_target_pairs={{0,3},{1,0},{2,1},{3,2},{4,7},{5,4},{6,5},{7,6},{8,11},{9,8},{10,9... | collective-permute-start | bytes 2359304 | tf_op jit(solution)/shard_map/ppermute | solution.py:42
  99.5 10.5 %copy-start.7 = (bf16[256,1536]{1,0:T(8,128)(2,1)}, bf16[256,1536]{1,0:T(8,128)(2,1)S(1)}, u32[]{:S(2)}) copy-start(bf16[256,1536]{1,0:T(8,128)(2,1)S(1)} %collective-permute-done.4.refs_3_) | copy-start | bytes 2359300
  99.5 37.7 %collective-permute-start.5 = (bf16[512,1536]{1,0:T(8,128)(2,1)}, bf16[512,1536]{1,0:T(8,128)(2,1)}, u32[]{:S(2)}, u32[]{:S(2)}) collective-permute-start(bf16[512,1536]{1,0:T(8,128)(2,1)} %collective-permute-done.refs_4_), channel_id=1, source_target_pairs={{0,1},{1,2},{2,3},{3,0},{4,5},{5,6},{6,7},{7,4},{8,9},{9,10},{10,1... | collective-permute-start | bytes 4718600 | tf_op jit(solution)/shard_map/ppermute | solution.py:37
  101.0 37.8 %collective-permute-start.7 = (bf16[512,1536]{1,0:T(8,128)(2,1)}, bf16[512,1536]{1,0:T(8,128)(2,1)}, u32[]{:S(2)}, u32[]{:S(2)}) collective-permute-start(bf16[512,1536]{1,0:T(8,128)(2,1)} %collective-permute-done.refs_4_), channel_id=1, source_target_pairs={{0,3},{1,0},{2,1},{3,2},{4,7},{5,4},{6,5},{7,6},{8,11},{9,8},{10,9... | collective-permute-start | bytes 4718600 | tf_op jit(solution)/shard_map/ppermute | solution.py:37
  110.0 57.0 %all-to-all-start.2 = ((bf16[8,96,2048]{2,1,0:T(8,128)(2,1)}), bf16[8,96,2048]{2,1,0:T(8,128)(2,1)S(1)}, u32[]{:S(2)}, u32[]{:S(2)}) async-start(bf16[8,96,2048]{2,1,0:T(8,128)(2,1)} %bitcast.47), calls=%async_computation.2 | async-start | bytes 6291456 | tf_op jit(solution)/shard_map/all_to_all | solution.py:227
  114.8 28.9 %copy-start.9 = (bf16[2,16,1536]{2,1,0:T(8,128)(2,1)S(1)}, bf16[2,16,1536]{2,1,0:T(8,128)(2,1)}, u32[]{:S(2)}) copy-start(bf16[2,16,1536]{2,1,0:T(8,128)(2,1)} %param.11) | copy-start | bytes 294916
  114.8 29.5 %copy-start.6 = (bf16[768,1536]{1,0:T(8,128)(2,1)S(1)}, bf16[768,1536]{1,0:T(8,128)(2,1)}, u32[]{:S(2)}) copy-start(bf16[768,1536]{1,0:T(8,128)(2,1)} %convolution_convert_fusion.4) | copy-start | bytes 7077892
  114.9 30.8 %copy-start.8 = (bf16[16,2048]{1,0:T(8,128)(2,1)}, bf16[16,2048]{1,0:T(8,128)(2,1)S(1)}, u32[]{:S(2)}) copy-start(bf16[16,2048]{1,0:T(8,128)(2,1)S(1)} %get-tuple-element.66.first_ref) | copy-start | bytes 196612
  114.9 30.8 %copy-start.10 = (bf16[16,2048]{1,0:T(8,128)(2,1)}, bf16[16,2048]{1,0:T(8,128)(2,1)S(1)}, u32[]{:S(2)}) copy-start(bf16[16,2048]{1,0:T(8,128)(2,1)S(1)} %get-tuple-element.67.first_ref) | copy-start | bytes 196612
  138.4 19.8 %collective-permute-start.6 = (bf16[256,1536]{1,0:T(8,128)(2,1)S(1)}, bf16[256,1536]{1,0:T(8,128)(2,1)S(1)}, u32[]{:S(2)}, u32[]{:S(2)}) collective-permute-start(bf16[256,1536]{1,0:T(8,128)(2,1)S(1)} %slice.142), channel_id=1, source_target_pairs={{0,1},{1,2},{2,3},{3,0},{4,5},{5,6},{6,7},{7,4},{8,9},{9,10},{10,1... | collective-permute-start | bytes 2359304 | tf_op jit(solution)/shard_map/ppermute | solution.py:42
  140.1 19.0 %collective-permute-start.8 = (bf16[256,1536]{1,0:T(8,128)(2,1)S(1)}, bf16[256,1536]{1,0:T(8,128)(2,1)}, u32[]{:S(2)}, u32[]{:S(2)}) collective-permute-start(bf16[256,1536]{1,0:T(8,128)(2,1)S(1)} %slice.143), channel_id=1, source_target_pairs={{0,3},{1,0},{2,1},{3,2},{4,7},{5,4},{6,5},{7,6},{8,11},{9,8},{10,9... | collective-permute-start | bytes 2359304 | tf_op jit(solution)/shard_map/ppermute | solution.py:42
  145.7 40.3 %collective-permute-start.10 = (bf16[96,1536]{1,0:T(8,128)(2,1)}, bf16[96,1536]{1,0:T(8,128)(2,1)}, u32[]{:S(2)}, u32[]{:S(2)}) collective-permute-start(bf16[96,1536]{1,0:T(8,128)(2,1)} %get-tuple-element.61), channel_id=1, source_target_pairs={{0,64},{4,68},{64,128},{68,132},{128,192},{132,196},{192,0},{196,4... | collective-permute-start | bytes 884744 | tf_op jit(solution)/shard_map/ppermute | solution.py:239
  159.1 22.9 %collective-permute-start.9 = (bf16[96,1536]{1,0:T(8,128)(2,1)}, bf16[96,1536]{1,0:T(8,128)(2,1)}, u32[]{:S(2)}, u32[]{:S(2)}) collective-permute-start(bf16[96,1536]{1,0:T(8,128)(2,1)} %get-tuple-element.42), channel_id=1, source_target_pairs={{0,4},{4,64},{64,68},{68,128},{128,132},{132,192},{192,196},{196,0... | collective-permute-start | bytes 884744 | tf_op jit(solution)/shard_map/ppermute | solution.py:239
  168.6 66.7 %all-to-all-start.3 = ((bf16[8,96,2048]{2,1,0:T(8,128)(2,1)}), bf16[8,96,2048]{2,1,0:T(8,128)(2,1)}, u32[]{:S(2)}, u32[]{:S(2)}) async-start(bf16[8,96,2048]{2,1,0:T(8,128)(2,1)} %bitcast.48), calls=%async_computation.3 | async-start | bytes 6291456 | tf_op jit(solution)/shard_map/all_to_all | solution.py:227
  174.7 28.4 %collective-permute-start.11 = (bf16[96,1536]{1,0:T(8,128)(2,1)}, bf16[96,1536]{1,0:T(8,128)(2,1)S(1)}, u32[]{:S(2)}, u32[]{:S(2)}) collective-permute-start(bf16[96,1536]{1,0:T(8,128)(2,1)} %get-tuple-element.43), channel_id=1, source_target_pairs={{0,132},{4,192},{64,196},{68,0},{128,4},{132,64},{192,68},{196,128... | collective-permute-start | bytes 884744 | tf_op jit(solution)/shard_map/ppermute | solution.py:239
  178.7 33.6 %collective-permute-start.12 = (bf16[96,1536]{1,0:T(8,128)(2,1)}, bf16[96,1536]{1,0:T(8,128)(2,1)S(1)}, u32[]{:S(2)}, u32[]{:S(2)}) collective-permute-start(bf16[96,1536]{1,0:T(8,128)(2,1)} %get-tuple-element.44), channel_id=1, source_target_pairs={{0,192},{4,196},{64,0},{68,4},{128,64},{132,68},{192,128},{196,132... | collective-permute-start | bytes 884744 | tf_op jit(solution)/shard_map/ppermute | solution.py:239
  182.0 37.1 %collective-permute-start.13 = (bf16[96,1536]{1,0:T(8,128)(2,1)}, bf16[96,1536]{1,0:T(8,128)(2,1)S(1)}, u32[]{:S(2)}, u32[]{:S(2)}) collective-permute-start(bf16[96,1536]{1,0:T(8,128)(2,1)} %get-tuple-element.45), channel_id=1, source_target_pairs={{0,196},{4,0},{64,4},{68,64},{128,68},{132,128},{192,132},{196,192... | collective-permute-start | bytes 884744 | tf_op jit(solution)/shard_map/ppermute | solution.py:239
  182.0 37.1 %collective-permute-start.14 = (bf16[96,1536]{1,0:T(8,128)(2,1)}, bf16[96,1536]{1,0:T(8,128)(2,1)S(1)}, u32[]{:S(2)}, u32[]{:S(2)}) collective-permute-start(bf16[96,1536]{1,0:T(8,128)(2,1)} %get-tuple-element.46), channel_id=1, source_target_pairs={{0,128},{4,132},{64,192},{68,196},{128,0},{132,4},{192,64},{196,68... | collective-permute-start | bytes 884744 | tf_op jit(solution)/shard_map/ppermute | solution.py:239
  186.1 34.0 %collective-permute-start.15 = (bf16[96,1536]{1,0:T(8,128)(2,1)}, bf16[96,1536]{1,0:T(8,128)(2,1)S(1)}, u32[]{:S(2)}, u32[]{:S(2)}) collective-permute-start(bf16[96,1536]{1,0:T(8,128)(2,1)} %get-tuple-element.47), channel_id=1, source_target_pairs={{0,68},{4,128},{64,132},{68,192},{128,196},{132,0},{192,4},{196,64... | collective-permute-start | bytes 884744 | tf_op jit(solution)/shard_map/ppermute | solution.py:239
  235.3 54.8 %copy-start.1 = (bf16[2,4096,16]{1,2,0:T(8,128)(2,1)S(1)}, bf16[2,4096,16]{1,2,0:T(8,128)(2,1)}, u32[]{:S(2)}) copy-start(bf16[2,4096,16]{1,2,0:T(8,128)(2,1)} %param.10) | copy-start | bytes 786436
  (2 other events, 2.5 us)
Sparse Core Ops, SparseCore 0:
  10.3 81.8 all-gather.2
  94.1 57.6 all-gather.4
